TPU v7x, 32 devices: a whole 2x2x4 slice. The times are simulated.
32 devices in a mesh: dp: 8 (over z, x), vocab: 4 (over y, core).
Axes of the slice: x: 2, y: 2, z: 4, core: 2. Of those that a mesh axis runs over, the one named last changes fastest.
Arguments:
- hidden_states: bfloat16 [1024, 3584], P('dp', 'vocab'), may hold values from -750 to 750, as said below
- head_weight: bfloat16 [152064, 3584], P(('dp', 'vocab')), may hold values from -0.09375 to 0.09375
- token_ids: int32 [1024], P('dp'), may hold values from 0 to 152063
- response_mask: int32 [1024], P('dp'), may hold values 0 or 1
- rollout_logprobs: float32 [1024], P('dp'), may hold values from -14 to -6
- advantages: float32 [1024], P('dp'), may hold values from -6 to 6
Outputs:
- logprobs: float32 [1024], P('dp')
- tis_weight: float32 [1024], P('dp')
- loss: float32 [], replicated
Inputs may be any that keep to these rules, and one draw needn't show every extreme that they name: `hidden_states`: hidden states; some rows may be far larger than others.
All inputs are finite; a program needn't handle non-finite values. No bound on the sum of `response_mask` on one device may be relied on, other than what follows from the above.
Results may differ from a plain program's by a relative error of at most 0.0003.
Values may be sent and summed in bfloat16 or wider, within the bound.
A program may use at most 128 MiB of HBM per device.

v0:
```python
import jax
import jax.numpy as jnp
from jax import lax
from jax.sharding import PartitionSpec as P


def shard_stats(logits, ids_block, columns):
    matched = columns[None, :] == ids_block[:, None]
    picked = jnp.sum(jnp.where(matched, logits, 0.0), axis=1)
    peak = jnp.max(logits, axis=1)
    total = jnp.sum(jnp.exp(logits - peak[:, None]), axis=1)
    return (peak, total, picked)


def token_terms(logp, rollout, advant, mask):
    weight = jnp.minimum(jnp.exp(logp - rollout), 2.0)
    counted = mask.astype(jnp.float32)
    loss_part = -jnp.sum(counted * weight * advant * logp)
    return (weight, loss_part, jnp.sum(counted))


def body(hidden_states, head_weight, token_ids, response_mask, rollout_logprobs, advantages):
    rows_local = token_ids.shape[0]
    vocab_local = head_weight.shape[0]
    offset = lax.axis_index(("dp", "vocab")) * vocab_local
    own_columns = lax.iota(jnp.int32, vocab_local) + offset
    dp_index = lax.axis_index("dp")
    own_start = dp_index * rows_local
    all_ids, all_mask = (
        lax.all_gather(token_ids, "dp", axis=0, tiled=True),
        lax.all_gather(response_mask, "dp", axis=0, tiled=True),
    )
    all_rollout, all_advant = (
        lax.all_gather(rollout_logprobs, "dp", axis=0, tiled=True),
        lax.all_gather(advantages, "dp", axis=0, tiled=True),
    )
    full_rows = lax.all_gather(hidden_states, "vocab", axis=1, tiled=True)
    logits = jnp.einsum(
        "rd,vd->rv",
        lax.all_gather(full_rows, "dp", axis=0, tiled=True),
        head_weight,
        preferred_element_type=jnp.float32,
    )
    peak, total, picked = shard_stats(logits, all_ids, own_columns)
    peak, total, picked = (peak, total, picked)
    top = lax.pmax(peak, ("dp", "vocab"))
    total_sum, picked_sum = lax.psum((total * jnp.exp(peak - top), picked), ("dp", "vocab"))
    logprob_all = picked_sum - (top + jnp.log(total_sum))
    own_logp = lax.dynamic_slice_in_dim(logprob_all, own_start, rows_local, 0)
    weight_all, loss_sum, count = token_terms(logprob_all, all_rollout, all_advant, all_mask)
    weight = lax.dynamic_slice_in_dim(weight_all, own_start, rows_local, 0)
    loss = loss_sum / jnp.maximum(count, 1.0)
    return (own_logp, weight, loss)


def solution(mesh):
    placed = (P("dp", "vocab"), P(("dp", "vocab"), None), P("dp"), P("dp"), P("dp"), P("dp"))
    return jax.shard_map(
        body, mesh=mesh, in_specs=placed, out_specs=(P("dp"), P("dp"), P()), check_vma=False
    )
```

profile of v0, /device:TPU:0, one launch (start us, length us, event | category | flops | bytes accessed | tf_op | source)
XLA Modules:
  0.0 274.0 jit_solution(17611963197525337187)
XLA Ops:
  7.2 0.0 all-gather.6.cloned.1.call-start
  7.2 12.5 %all_gather.19 = bf16[128,3584]{1,0:T(8,128)(2,1)} all-gather(bf16[128,896]{1,0:T(8,128)(2,1)} %param.6), channel_id=1, replica_groups=mesh['dp'=8,'vocab'=4] {'vocab'}, dimensions={1}, use_global_device_ids=true | all-gather | bytes 1146880 | tf_op jit(solution)/shard_map/all_gather | solution.py:37
  19.7 0.0 all-gather.6.cloned.1.call-update
  19.7 21.4 %all-gather.2 = s32[8,1,128]{2,1,0:T(1,128)S(1)} all-gather(s32[1,1,128]{2,1,0:T(1,128)} %bitcast.15), channel_id=1, replica_groups=mesh['dp'=8,'vocab'=4] {'dp'}, dimensions={0}, use_global_device_ids=true | all-gather | bytes 4608 | tf_op jit(solution)/shard_map/all_gather | solution.py:31
  41.2 0.6 convert_reduce_fusion
  42.4 17.1 %all-gather = s32[8,1,128]{2,1,0:T(1,128)S(1)} all-gather(s32[1,1,128]{2,1,0:T(1,128)} %bitcast.16), channel_id=1, replica_groups=mesh['dp'=8,'vocab'=4] {'dp'}, dimensions={0}, use_global_device_ids=true | all-gather | bytes 4608 | tf_op jit(solution)/shard_map/all_gather | solution.py:30
  59.5 18.8 %all-gather.1 = f32[8,1,128]{2,1,0:T(1,128)S(1)} all-gather(f32[1,1,128]{2,1,0:T(1,128)} %bitcast.17), channel_id=1, replica_groups=mesh['dp'=8,'vocab'=4] {'dp'}, dimensions={0}, use_global_device_ids=true | all-gather | bytes 4608 | tf_op jit(solution)/shard_map/all_gather | solution.py:34
  78.3 17.3 %all-gather.3 = f32[8,1,128]{2,1,0:T(1,128)S(1)} all-gather(f32[1,1,128]{2,1,0:T(1,128)} %bitcast.18), channel_id=1, replica_groups=mesh['dp'=8,'vocab'=4] {'dp'}, dimensions={0}, use_global_device_ids=true | all-gather | bytes 4608 | tf_op jit(solution)/shard_map/all_gather | solution.py:35
  95.6 36.2 %all-gather.6.cloned.1.call-done = bf16[1024,3584]{1,0:T(8,128)(2,1)} async-done(((bf16[128,3584]{1,0:T(8,128)(2,1)}), bf16[1024,3584]{1,0:T(8,128)(2,1)}) %all-gather.6.cloned.1.call-update) | async-done | bytes 7340048 | tf_op jit(solution)/shard_map/all_gather | solution.py:40
  131.8 43.0 %fusion = (f32[1024]{0:T(1024)S(1)}, f32[1024,4752]{0,1:T(8,128)}) fusion(bf16[1024,3584]{1,0:T(8,128)(2,1)} %all-gather.6.cloned.1.call-done, bf16[4752,3584]{1,0:T(8,128)(2,1)} %param.7), kind=kOutput, calls=%fused_computation.8 | convolution fusion | flops 34884698112 | bytes 60870656 | tf_op jit(solution)/shard_map/rd,vd->rv/dot_general | solution.py:38
  174.8 38.4 %pmax.7 = f32[1024]{0:T(1024)S(1)} all-reduce(f32[1024]{0:T(1024)S(1)} %get-tuple-element.9), channel_id=1, replica_groups=mesh['dp'=8,'vocab'=4] {'dp','vocab'}, use_global_device_ids=true, to_apply=%region_3.4 | all-reduce | flops 1024 | bytes 8192 | tf_op jit(solution)/shard_map/pmax | solution.py:46
  213.1 9.5 %exponential_reduce_fusion = (f32[1024]{0:T(1024)S(1)}, f32[1024]{0:T(1024)S(1)}) fusion(f32[1024,4752]{0,1:T(8,128)} %get-tuple-element.10, f32[1024]{0:T(1024)S(1)} %get-tuple-element.9, s32[1024]{0:T(1024)S(1)} %bitcast.14, s32[4752]{0:T(1024)S(1)} %iota_add_fusion), kind=kLoop, calls=%fused_computation | loop fusion | flops 24328192 | bytes 19499584 | tf_op jit(solution)/shard_map/reduce_sum | solution.py:11
  222.7 40.8 %all-reduce = (f32[1024]{0:T(1024)S(1)}, f32[1024]{0:T(1024)S(1)}) all-reduce(f32[1024]{0:T(1024)S(1)} %get-tuple-element.4, f32[1024]{0:T(1024)S(1)} %exponential_multiply_fusion), channel_id=1, replica_groups=mesh['dp'=8,'vocab'=4] {'dp','vocab'}, use_global_device_ids=true, to_apply=%region_1.2 | all-reduce | flops 2048 | bytes 16384 | tf_op jit(solution)/shard_map/psum | solution.py:47
  263.5 0.6 multiply_reduce_fusion
  264.1 0.6 dynamic_slice.6
  264.7 0.6 dynamic_slice.7
  (4 shorter events, 0.0 us)
Async XLA Ops:
  7.2 124.6 %all-gather.6.cloned.1.call-start = ((), (), s32[]{:S(2)}) async-start(), calls=%async_computation | async-start | bytes 8257536 | tf_op jit(solution)/shard_map/all_gather | solution.py:40
Sparse Core Ops, SparseCore 0:
  19.8 111.9 all-gather.5
where the time goes:
time: 275 us; the launch traced here: 274 us
  blocking collectives  166 us (60%)
  matrix products  43 us (16%)
  waiting for transfers between devices  36.2 us (13%)
  between operations  16.5 us (6%)
  other arithmetic  10.8 us (4%)
    dot_general x1, matrix products, body(): jnp.einsum('rd,vd->rv', lax.all_gather(full_rows, 'dp', axis=0, tiled=Tru...  43 us
    psum x1, blocking collectives, body(): lax.psum((total * jnp.exp(peak - top), picked), ('dp', 'vocab'))  40.8 us
    pmax x1, blocking collectives, body(): top = lax.pmax(peak, ('dp', 'vocab'))  38.4 us
    all_gather x1, waiting for transfers between devices, body(): lax.all_gather(full_rows, 'dp', axis=0, tiled=True)  36.2 us
    all_gather x1, blocking collectives, body(): lax.all_gather(response_mask, 'dp', axis=0, tiled=True)  21.4 us
    all_gather x1, blocking collectives, body(): lax.all_gather(rollout_logprobs, 'dp', axis=0, tiled=True)  18.8 us
    all_gather x1, blocking collectives, body(): lax.all_gather(advantages, 'dp', axis=0, tiled=True)  17.3 us
    all_gather x1, blocking collectives, body(): lax.all_gather(token_ids, 'dp', axis=0, tiled=True)  17.1 us
  transfers between devices with their start and end apart: 1, of which 1 were waited for; matrix products, arithmetic and copies ran while one was open for 0% of the time, Pallas kernels for 0%

commit v1 on v0

--- a/solution.py
+++ b/solution.py
@@ -44,7 +44,13 @@
     peak, total, picked = shard_stats(logits, all_ids, own_columns)
     peak, total, picked = (peak, total, picked)
     top = lax.pmax(peak, ("dp", "vocab"))
-    total_sum, picked_sum = lax.psum((total * jnp.exp(peak - top), picked), ("dp", "vocab"))
+
+    def _try_all_shards(field_in):
+        for i0 in ("vocab", "dp"):
+            field_in = lax.psum(field_in, axis_name=i0)
+        return field_in
+
+    total_sum, picked_sum = _try_all_shards((total * jnp.exp(peak - top), picked))
     logprob_all = picked_sum - (top + jnp.log(total_sum))
     own_logp = lax.dynamic_slice_in_dim(logprob_all, own_start, rows_local, 0)
     weight_all, loss_sum, count = token_terms(logprob_all, all_rollout, all_advant, all_mask)

time: 275 us -> 261 us (0.949)
  blocking collectives: 166 us -> 153 us
    psum x1 -> x2, blocking collectives: 40.8 us -> 27.1 us  [_try_all_shards(): field_in = lax.psum(field_in, axis_name=i0)]
where the time goes in v1:
time: 261 us; the launch traced here: 260 us
  blocking collectives  153 us (59%)
  matrix products  43 us (16%)
  waiting for transfers between devices  36.2 us (14%)
  between operations  16.5 us (6%)
  other arithmetic  10.8 us (4%)
    dot_general x1, matrix products, body(): jnp.einsum('rd,vd->rv', lax.all_gather(full_rows, 'dp', axis=0, tiled=Tru...  43 us
    pmax x1, blocking collectives, body(): top = lax.pmax(peak, ('dp', 'vocab'))  38.3 us
    all_gather x1, waiting for transfers between devices, body(): lax.all_gather(full_rows, 'dp', axis=0, tiled=True)  36.2 us
    psum x2, blocking collectives, _try_all_shards(): field_in = lax.psum(field_in, axis_name=i0)  27.1 us
    all_gather x1, blocking collectives, body(): lax.all_gather(response_mask, 'dp', axis=0, tiled=True)  21.4 us
    all_gather x1, blocking collectives, body(): lax.all_gather(rollout_logprobs, 'dp', axis=0, tiled=True)  18.8 us
    all_gather x1, blocking collectives, body(): lax.all_gather(advantages, 'dp', axis=0, tiled=True)  17.3 us
    all_gather x1, blocking collectives, body(): lax.all_gather(token_ids, 'dp', axis=0, tiled=True)  17.1 us
  transfers between devices with their start and end apart: 1, of which 1 were waited for; matrix products, arithmetic and copies ran while one was open for 0% of the time, Pallas kernels for 0%

profile of v1, /device:TPU:0, one launch (start us, length us, event | category | flops | bytes accessed | tf_op | source)
XLA Modules:
  0.0 260.3 jit_solution(4974173748120706496)
XLA Ops:
  7.2 0.0 all-gather.6.cloned.1.call-start
  7.2 12.5 %all_gather.19 = bf16[128,3584]{1,0:T(8,128)(2,1)} all-gather(bf16[128,896]{1,0:T(8,128)(2,1)} %param.6), channel_id=1, replica_groups=mesh['dp'=8,'vocab'=4] {'vocab'}, dimensions={1}, use_global_device_ids=true | all-gather | bytes 1146880 | tf_op jit(solution)/shard_map/all_gather | solution.py:37
  19.7 0.0 all-gather.6.cloned.1.call-update
  19.7 21.4 %all-gather.2 = s32[8,1,128]{2,1,0:T(1,128)S(1)} all-gather(s32[1,1,128]{2,1,0:T(1,128)} %bitcast.15), channel_id=1, replica_groups=mesh['dp'=8,'vocab'=4] {'dp'}, dimensions={0}, use_global_device_ids=true | all-gather | bytes 4608 | tf_op jit(solution)/shard_map/all_gather | solution.py:31
  41.2 0.6 convert_reduce_fusion
  42.4 17.1 %all-gather = s32[8,1,128]{2,1,0:T(1,128)S(1)} all-gather(s32[1,1,128]{2,1,0:T(1,128)} %bitcast.16), channel_id=1, replica_groups=mesh['dp'=8,'vocab'=4] {'dp'}, dimensions={0}, use_global_device_ids=true | all-gather | bytes 4608 | tf_op jit(solution)/shard_map/all_gather | solution.py:30
  59.5 18.8 %all-gather.1 = f32[8,1,128]{2,1,0:T(1,128)S(1)} all-gather(f32[1,1,128]{2,1,0:T(1,128)} %bitcast.17), channel_id=1, replica_groups=mesh['dp'=8,'vocab'=4] {'dp'}, dimensions={0}, use_global_device_ids=true | all-gather | bytes 4608 | tf_op jit(solution)/shard_map/all_gather | solution.py:34
  78.3 17.3 %all-gather.3 = f32[8,1,128]{2,1,0:T(1,128)S(1)} all-gather(f32[1,1,128]{2,1,0:T(1,128)} %bitcast.18), channel_id=1, replica_groups=mesh['dp'=8,'vocab'=4] {'dp'}, dimensions={0}, use_global_device_ids=true | all-gather | bytes 4608 | tf_op jit(solution)/shard_map/all_gather | solution.py:35
  95.6 36.2 %all-gather.6.cloned.1.call-done = bf16[1024,3584]{1,0:T(8,128)(2,1)} async-done(((bf16[128,3584]{1,0:T(8,128)(2,1)}), bf16[1024,3584]{1,0:T(8,128)(2,1)}) %all-gather.6.cloned.1.call-update) | async-done | bytes 7340048 | tf_op jit(solution)/shard_map/all_gather | solution.py:40
  131.8 43.0 %fusion = (f32[1024]{0:T(1024)S(1)}, f32[1024,4752]{0,1:T(8,128)}) fusion(bf16[1024,3584]{1,0:T(8,128)(2,1)} %all-gather.6.cloned.1.call-done, bf16[4752,3584]{1,0:T(8,128)(2,1)} %param.7), kind=kOutput, calls=%fused_computation.8 | convolution fusion | flops 34884698112 | bytes 60870656 | tf_op jit(solution)/shard_map/rd,vd->rv/dot_general | solution.py:38
  174.8 38.3 %pmax.7 = f32[1024]{0:T(1024)S(1)} all-reduce(f32[1024]{0:T(1024)S(1)} %get-tuple-element.11), channel_id=1, replica_groups=mesh['dp'=8,'vocab'=4] {'dp','vocab'}, use_global_device_ids=true, to_apply=%region_4.5 | all-reduce | flops 1024 | bytes 8192 | tf_op jit(solution)/shard_map/pmax | solution.py:46
  213.1 9.5 %exponential_reduce_fusion = (f32[1024]{0:T(1024)S(1)}, f32[1024]{0:T(1024)S(1)}) fusion(f32[1024,4752]{0,1:T(8,128)} %get-tuple-element.12, f32[1024]{0:T(1024)S(1)} %get-tuple-element.11, s32[1024]{0:T(1024)S(1)} %bitcast.14, s32[4752]{0:T(1024)S(1)} %iota_add_fusion), kind=kLoop, calls=%fused_computation | loop fusion | flops 24328192 | bytes 19499584 | tf_op jit(solution)/shard_map/reduce_sum | solution.py:11
  222.7 6.7 %all-reduce.1 = (f32[1024]{0:T(1024)S(1)}, f32[1024]{0:T(1024)S(1)}) all-reduce(f32[1024]{0:T(1024)S(1)} %get-tuple-element.4, f32[1024]{0:T(1024)S(1)} %exponential_multiply_fusion), channel_id=1, replica_groups=mesh['dp'=8,'vocab'=4] {'vocab'}, use_global_device_ids=true, to_apply=%region_1.2 | all-reduce | flops 2048 | bytes 16384 | tf_op jit(solution)/shard_map/psum | solution.py:50
  229.3 20.5 %all-reduce = (f32[1024]{0:T(1024)S(1)}, f32[1024]{0:T(1024)S(1)}) all-reduce(f32[1024]{0:T(1024)S(1)} %get-tuple-element.7, f32[1024]{0:T(1024)S(1)} %get-tuple-element.8), channel_id=1, replica_groups=mesh['dp'=8,'vocab'=4] {'dp'}, use_global_device_ids=true, to_apply=%region_2.3 | all-reduce | flops 2048 | bytes 16384 | tf_op jit(solution)/shard_map/psum | solution.py:50
  249.8 0.6 multiply_reduce_fusion
  250.4 0.6 dynamic_slice.6
  251.0 0.6 dynamic_slice.7
  (4 shorter events, 0.0 us)
Async XLA Ops:
  7.2 124.6 %all-gather.6.cloned.1.call-start = ((), (), s32[]{:S(2)}) async-start(), calls=%async_computation | async-start | bytes 8257536 | tf_op jit(solution)/shard_map/all_gather | solution.py:40
Sparse Core Ops, SparseCore 0:
  19.8 111.9 all-gather.5
